TPU v7x, 512 devices: a 8x2x16 block of a 8x8x16 slice. The times are simulated.
512 devices in a mesh: groups: 2 (over y), tensor: 32 (over z, core), section: 8 (over x).
Axes of the slice: x: 8, y: 2, z: 16, core: 2. Of those that a mesh axis runs over, the one named last changes fastest.
The devices are a block of a 8x8x16 slice.
Arguments:
- hidden: bfloat16 [128, 8192], P('groups', 'tensor'), parts along dimension 0, may hold values from -6 to 6
- norm_gain: bfloat16 [8, 8192], P('section'), may hold values from 0.5 to 1.5
- query_weight: bfloat16 [8, 8192, 4096], P('section', None, 'tensor'), may hold values from -0.0625 to 0.0625
- query_bias: bfloat16 [8, 4096], P('section', 'tensor'), may hold values from -10 to 10
- kv_weight: bfloat16 [8, 8192, 1024], P('section', None, 'tensor'), may hold values from -0.0625 to 0.0625
- out_weight: bfloat16 [8, 4096, 8192], P('section', None, 'tensor'), may hold values from -0.09375 to 0.09375
- kv_pool: bfloat16 [8, 384, 16, 1024], P('section', ('groups', 'tensor')), parts along dimension 1, may hold values from -8 to 8
- page_table: int32 [128, 4], P(('groups', 'tensor')), parts along dimension 0, may hold values from 0 to 191, as said below
- context_len: int32 [128], P(('groups', 'tensor')), parts along dimension 0, may hold values from 33 to 64, as said below
Outputs:
- result: bfloat16 [128, 8192], P(('groups', 'section'), 'tensor'), parts along dimension 0
There are 2 independent parts, one for each index of `groups`. A program takes and returns all parts, laid end to end along the dimension named above; an argument that names none is the same for every part. Nothing has to cross between parts.
Inputs may be any that keep to these rules, and one draw needn't show every extreme that they name: `page_table`: sample r belongs to block k = r // 2; its 4 pages lie in k * 6 to (k + 1) * 6 - 1. The first 2 pages are the same for all samples of a block, every other page belongs to one sample only. `context_len`: some sample has 64 cached tokens.
All inputs are finite; a program needn't handle non-finite values.
Results may differ from a plain program's by a relative error of at most 0.018.
Values may be sent and summed in bfloat16 or wider, within the bound.
A program may use at most 64 MiB of HBM per device.

v0:
```python
import functools

import jax
import jax.numpy as jnp
from jax import lax
from jax.experimental import pallas as pl
from jax.experimental.pallas import tpu as pltpu
from jax.sharding import PartitionSpec as P

MESH = pl.DeviceIdType.MESH
EPSILON = 1e-06
LOG_ROPE_BASE = 13.815510557964274
BF16 = jnp.bfloat16
F32 = jnp.float32


def relay_tree(half):
    far = half // 2
    return {d: 0 if d <= far else far for d in range(1, half + 1)}


def kernel(
    nc,
    nsec,
    hidden_hbm,
    gain_hbm,
    wq_hbm,
    bias_hbm,
    wkv_hbm,
    wo_hbm,
    pool_hbm,
    table_ref,
    len_ref,
    out_ref,
    hid,
    gain_in,
    gain,
    wq,
    bias,
    wkv,
    wo,
    pool,
    keys,
    values,
    cos_tab,
    sin_tab,
    lim_tab,
    first,
    xbuf,
    qkv_out,
    qkv_in,
    mix_own,
    mixbuf,
    stream,
    load_sems,
    push_send,
    push_recv,
    x_send,
    x_recv,
    i_send,
    r_send,
    a2a_send,
    a2a_recv,
    m_send,
    m_root,
    m_recv,
    out_send,
    out_recv,
    ready,
    turn,
):
    row_dev, blocks = table_ref.shape
    width = hid.shape[2]
    rows = nc * row_dev
    hd = keys.shape[1]
    heads = mix_own.shape[0]
    page_len = pool.shape[1]
    span = page_len * blocks
    wide = keys.shape[0]
    kvh = wide // row_dev // span
    per_chip = heads // nc
    part = wkv.shape[0]
    half = nc // 2
    parent = relay_tree(half)
    kids = {d: sorted((c for c in parent if parent[c] == d), reverse=True) for d in range(half + 1)}
    far = half // 2
    near = [(s, d) for d in range(far, 0, -1) for s in (1, -1)] + [(1, 0)]

    me = lax.axis_index("tensor")
    sec = lax.axis_index("section")
    z = me // 2
    core = lax.rem(me, 2)
    last = nsec - 1

    def dev(zz, s=None):
        where = {"tensor": lax.rem(zz + 2 * nc, nc) * 2 + core}
        if s is not None:
            where["section"] = s
        return where

    def put(src, dst, ssem, rsem, where):
        copy = pltpu.make_async_remote_copy(
            src_ref=src, dst_ref=dst, send_sem=ssem, recv_sem=rsem, device_id=where, device_id_type=MESH
        )
        copy.start()
        return copy

    def wait_for(ref, sem):
        pltpu.make_async_copy(ref, ref, sem).wait()

    def cut(ref, axis, c):
        n = ref.shape[axis] // 2
        at = pl.multiple_of(c * n, n)
        return ref.at[pl.ds(at, n)] if axis == 0 else ref.at[:, pl.ds(at, n)]

    def shares(c):
        return [hid.at[c], bias.at[c], cut(wq, 1, c), cut(wkv, 0, c), cut(wo, 1, c)]

    sources = [hidden_hbm, bias_hbm, wq_hbm, wkv_hbm, wo_hbm]

    def load(k, src, dst):
        copy = pltpu.make_async_copy(src, dst, load_sems.at[k])
        copy.start()
        return copy

    load_gain, load_pool = load(0, gain_hbm, gain_in), load(1, pool_hbm, pool)
    own_loads = [load(2 + k, src, dst) for k, (src, dst) in enumerate(zip(sources, shares(core)))]

    barrier = pltpu.get_barrier_semaphore()

    def greet(where):
        pl.semaphore_signal(barrier, inc=1, device_id=where, device_id_type=MESH)

    sibling = {"tensor": z * 2 + 1 - core}
    greet(sibling)

    @pl.loop(1, nc)
    def _(i):
        greet(dev(z + i))

    @pl.when(sec < last)
    def _():
        for s, d in near:
            greet(dev(z + s * d, sec + 1))

    @pl.when(sec > 0)
    def _():
        pl.semaphore_wait(barrier, nc + len(near))
        for s, d in near:
            pl.semaphore_signal(ready, inc=1, device_id=dev(z - s * d, sec - 1), device_id_type=MESH)

    @pl.when(sec == 0)
    def _():
        pl.semaphore_wait(barrier, nc)

    pushes = [
        put(src, dst, push_send.at[k], push_recv.at[k], sibling)
        for k, (src, dst) in enumerate(zip(sources, shares(core)))
    ]

    def send_stream(src, section, sems):
        return [
            put(src, xbuf.at[z], sems.at[k], x_recv.at[z], dev(z + s * d, section) if d else dev(z, section))
            for k, (s, d) in enumerate(near)
        ]

    own_loads[0].wait()
    wait_for(hid.at[0], push_recv.at[0])

    @pl.when(jnp.logical_and(sec == 0, core == 1))
    def _():
        pl.semaphore_wait(turn, 1)

    @pl.when(sec == 0)
    def _():
        whole = 2 * rows
        at = lax.broadcasted_iota(jnp.int32, (rows, whole), 0)
        col = lax.broadcasted_iota(jnp.int32, (rows, whole), 1)
        row = (at // row_dev * 2 + core) * row_dev + lax.rem(at, row_dev)
        pick = jnp.where(col == row, 1.0, 0.0).astype(BF16)
        for c in range(2):
            first[c] = jnp.dot(pick, hid[c], preferred_element_type=F32).astype(BF16)
        for k, (s, d) in enumerate(near):
            if d:
                put(first, xbuf.at[z], i_send.at[k], x_recv.at[z], dev(z + s * d))
            else:
                pltpu.make_async_copy(first, xbuf.at[z], x_recv.at[z]).start()

    load_gain.wait()
    for t in range(2 * nc):
        gain[t] = gain_in[:, t * width : (t + 1) * width].astype(F32)
    load_pool.wait()
    for r in range(row_dev):
        for b in range(blocks):
            page = pool[lax.rem(table_ref[r, b], pool.shape[0])]
            for k in range(kvh):
                at = (r * kvh + k) * span + b * page_len
                keys[at : at + page_len, :] = page[:, k * hd : (k + 1) * hd]
                values[at : at + page_len, :] = page[:, (kvh + k) * hd : (kvh + k + 1) * hd]

    q_rows = per_chip * rows
    lane = lax.broadcasted_iota(jnp.int32, (q_rows, hd), 1)
    sample = lax.rem(lax.broadcasted_iota(jnp.int32, (q_rows, hd), 0), row_dev)
    position = jnp.full((q_rows, hd), len_ref[0], jnp.int32)
    for r in range(1, row_dev):
        position = jnp.where(sample == r, len_ref[r], position)
    position = position.astype(F32)
    frequency = jnp.exp(lax.rem(lane, hd // 2).astype(F32) * (-2.0 * LOG_ROPE_BASE / hd))
    angle = position * frequency
    sine = jnp.sin(angle)
    cos_tab[...] = jnp.cos(angle)
    sin_tab[...] = jnp.where(lane < hd // 2, -sine, sine)
    lim_tab[...] = position
    for k in range(1, 4):
        own_loads[k].wait()
        wait_for(shares(0)[k], push_recv.at[k])

    def chip_at(d, s):
        return lax.rem(z - s * d + nc, nc)

    def in_half(ref, s):
        n = ref.shape[0] // 2
        return ref.at[pl.ds(0 if s == 1 else n, n)]

    def arrivals(known):
        at = dict(known)
        for d in sorted(parent):
            if d not in at:
                at[d] = at[parent[d]] + 1.7 + 0.6 * (d - parent[d])
        return at

    ring = [(d, s) for d in range(1, half) for s in (1, -1)] + [(half, 1)]

    def relay(place, recv, sems, items, skip, use):
        sent = []
        for _, d, s in sorted(items):
            chip = chip_at(d, s)
            block = place(chip)
            wait_for(block, recv.at[chip])
            for way in (1, -1) if d == 0 else (s,):
                for c in kids[d]:
                    if (d, c) not in skip:
                        piece = in_half(block, way) if c == half else block
                        sent.append(
                            put(piece, piece, sems.at[len(sent)], recv.at[chip], dev(z + way * (c - d)))
                        )
            use(chip)
        return sent

    sums = {
        "q": jnp.zeros((rows, per_chip * hd), F32),
        "kv": jnp.zeros((rows, part), F32),
        "squares": jnp.zeros((rows, width), F32),
    }

    def project(chip):
        parts = []
        for c in range(2):
            x = xbuf[chip, c].astype(F32)
            sums["squares"] += x * x
            parts.append((x * gain[chip * 2 + c]).astype(BF16))
        y = jnp.concatenate(parts, axis=1)
        at = pl.multiple_of(chip * 2 * width, 2 * width)
        sums["q"] += jnp.dot(y, wq[pl.ds(at, 2 * width), :], preferred_element_type=F32)
        sums["kv"] += lax.dot_general(
            y, wkv[:, pl.ds(at, 2 * width)], (((1,), (1,)), ((), ())), preferred_element_type=F32
        )

    due = arrivals({d: 1.7 + 0.6 * d for d in range(far + 1)})
    direct = {(0, d) for d in range(1, far + 1)}
    x_sent = relay(
        lambda c: xbuf.at[c], x_recv, x_send, [(due[d], d, s) for d, s in [(0, 1)] + ring], direct, project
    )

    @pl.when(jnp.logical_and(sec == 0, core == 0))
    def _():
        pl.semaphore_signal(turn, inc=1, device_id=sibling, device_id_type=MESH)

    def mine(ref, c):
        return ref.at[:, pl.ds(c * row_dev, row_dev)]

    scale = lax.rsqrt(jnp.sum(sums["squares"], axis=1, keepdims=True) / (2 * nc * width) + EPSILON)
    for i in range(per_chip):
        q = sums["q"][:, i * hd : (i + 1) * hd] * scale + bias[i].astype(F32)
        qkv_out[i] = q.astype(BF16)
    kv = (sums["kv"] * scale).astype(BF16).astype(F32)
    kv = jnp.concatenate([kv, jnp.zeros((rows, hd - part), F32)], axis=1)
    kv = pltpu.roll(kv, lax.rem(z, hd // part) * part, 1)
    qkv_out[per_chip] = kv.astype(BF16)

    @pl.loop(0, nc - 1)
    def _(i):
        c = lax.rem(z + half + (1 - 2 * lax.rem(i, 2)) * ((i + 1) // 2) + nc, nc)
        put(mine(qkv_out, c), mine(qkv_in, z), a2a_send, a2a_recv, dev(c))

    pltpu.make_async_copy(mine(qkv_out, z), mine(qkv_in, z), a2a_recv).start()

    def grid(shape, axis):
        return lax.broadcasted_iota(jnp.int32, shape, axis)

    group = heads // kvh
    q_of, c_of = grid((q_rows, wide), 0), grid((q_rows, wide), 1)
    key_head = (lax.rem(q_of, rows) // row_dev * per_chip + q_of // rows) // group
    matching = c_of // span == lax.rem(q_of, row_dev) * kvh + key_head
    usable = matching & (lax.rem(c_of, span).astype(F32) < lim_tab[:, :1])
    s_row, s_col = grid((q_rows, rows), 0), grid((q_rows, rows), 1)
    same = lax.rem(s_row, row_dev) == lax.rem(s_col, row_dev)
    source = s_col // row_dev // (hd // part)
    wanted = (lax.rem(s_row, rows) // row_dev * per_chip + s_row // rows) // group
    pick_key = jnp.where(same & (source == wanted), 1.0, 0.0).astype(BF16)
    pick_value = jnp.where(same & (source == wanted + kvh), 1.0, 0.0).astype(BF16)
    root = hd ** (-0.5)
    cos, sin = cos_tab[...], sin_tab[...]
    wait_for(qkv_in, a2a_recv)

    def rotate(v):
        return (v * cos + pltpu.roll(v, hd // 2, 1) * sin).astype(BF16)

    rotated = rotate(jnp.concatenate([qkv_in[i].astype(F32) for i in range(per_chip)], axis=0))
    fresh = qkv_in[per_chip]
    key_new = rotate(jnp.dot(pick_key, fresh, preferred_element_type=F32))
    value_new = jnp.dot(pick_value, fresh, preferred_element_type=F32)
    scores = lax.dot_general(rotated, keys[...], (((1,), (1,)), ((), ())), preferred_element_type=F32) * root
    own_score = jnp.sum(rotated.astype(F32) * key_new.astype(F32), axis=1, keepdims=True) * root
    top = jnp.maximum(jnp.max(jnp.where(usable, scores, -1e30), axis=1, keepdims=True), own_score)
    weights = jnp.where(usable, jnp.exp(scores - top), 0.0)
    own_weight = jnp.exp(own_score - top)
    total = jnp.sum(weights, axis=1, keepdims=True) + own_weight
    weights = (weights / total).astype(BF16)
    own_weight = (own_weight / total).astype(BF16).astype(F32)
    mixture = jnp.dot(weights, values[...], preferred_element_type=F32) + own_weight * value_new
    mix_own[...] = mixture.astype(BF16).reshape(heads, row_dev, hd)

    def mix_place(c):
        return mixbuf.at[:, c]

    m_sent = []
    for c in kids[0]:
        for s in (1, -1):
            m_sent.append(put(mix_own, mix_place(z), m_root.at[len(m_sent)], m_recv.at[z], dev(z + s * c)))
    pltpu.make_async_copy(mix_own, mix_place(z), m_recv.at[z]).start()
    due = arrivals({0: 0.0})
    m_sent += relay(mix_place, m_recv, m_send, [(due[d], d, s) for d, s in ring], {}, lambda c: None)
    wait_for(mix_place(z), m_recv.at[z])

    own_loads[4].wait()
    wait_for(shares(0)[4], push_recv.at[4])

    mixed = [mixbuf[i * nc + c].reshape(rows, hd) for c in range(nc) for i in range(per_chip)]
    change = jnp.dot(jnp.concatenate(mixed, axis=1), wo[...], preferred_element_type=F32)
    for c in range(2):
        x = xbuf[z, c].astype(F32)
        stream[c] = (x + change[:, c * width : (c + 1) * width]).astype(BF16)

    chips = nc // nsec

    @pl.when(sec < last)
    def _():
        pl.semaphore_wait(ready, len(near))
        for copy in send_stream(stream, sec + 1, r_send):
            copy.wait_send()

    @pl.when(sec == last)
    def _():
        def share(s, c, j):
            return (
                stream.at[c, pl.ds((s * chips + j) * row_dev, row_dev)],
                out_ref.at[pl.ds((j * 2 + core) * row_dev, row_dev)],
            )

        def sem_of(s, c, j):
            return out_send.at[(j * 2 + c) * nsec + s]

        for j in range(chips):
            for c in range(2):

                @pl.loop(0, last)
                def _(s):
                    put(*share(s, c, j), sem_of(s, c, j), out_recv, {"section": s, "tensor": z * 2 + c})

                @pl.when(core == c)
                def _():
                    pltpu.make_async_copy(*share(last, c, j), out_recv).start()

                @pl.when(core != c)
                def _():
                    put(*share(last, c, j), sem_of(last, c, j), out_recv, sibling)

        for j in range(chips):
            for c in range(2):

                @pl.loop(0, last)
                def _(s):
                    wait_for(stream.at[0, pl.ds(0, row_dev)], sem_of(s, c, j))

                @pl.when(core != c)
                def _():
                    wait_for(stream.at[0, pl.ds(0, row_dev)], sem_of(last, c, j))

    @pl.when(sec == 0)
    def _():
        for k, (s, d) in enumerate(near):
            if d:
                wait_for(first, i_send.at[k])

    others = pl.ds(0, rows - row_dev)
    wait_for(qkv_out.at[:, others], a2a_send)
    for copy in pushes + x_sent + m_sent:
        copy.wait_send()
    wait_for(out_ref, out_recv)


def solution(mesh):
    nc, nsec = mesh.shape["tensor"] // 2, mesh.shape["section"]

    def step(hidden, norm_gain, query_weight, query_bias, kv_weight, out_weight, kv_pool, page_table, context_len):
        all_rows, width = hidden.shape
        features, hd = query_weight.shape[1:]
        pages, page_len, kv_width = kv_pool.shape[1:]
        row_dev, blocks = page_table.shape
        part = 2 * kv_weight.shape[2]
        kvh = kv_width // (2 * hd)
        cached = row_dev * kvh * blocks * page_len
        heads = 2 * nc
        rows = all_rows // 2
        q_rows = rows * heads // nc
        anywhere = pl.BlockSpec(memory_space=pl.ANY)
        scalars = pl.BlockSpec(memory_space=pltpu.SMEM)
        dma = pltpu.SemaphoreType.DMA
        vmem = pltpu.VMEM
        return pl.pallas_call(
            functools.partial(kernel, nc, nsec),
            out_shape=jax.ShapeDtypeStruct((all_rows // nsec, width), BF16),
            in_specs=[anywhere] * 7 + [scalars] * 2,
            out_specs=pl.BlockSpec(memory_space=vmem),
            scratch_shapes=[
                vmem((2, all_rows, width), BF16),
                vmem((1, features), BF16),
                vmem((2 * nc, 1, width), F32),
                vmem((features, 2 * hd), BF16),
                vmem((2, 1, hd), BF16),
                vmem((part, features), BF16),
                vmem((heads * hd, 2 * width), BF16),
                vmem((pages, page_len, kv_width), BF16),
                vmem((cached, hd), BF16),
                vmem((cached, hd), BF16),
                vmem((q_rows, hd), F32),
                vmem((q_rows, hd), F32),
                vmem((q_rows, hd), F32),
                vmem((2, rows, width), BF16),
                vmem((nc, 2, rows, width), BF16),
                vmem((3, rows, hd), BF16),
                vmem((3, rows, hd), BF16),
                vmem((heads, row_dev, hd), BF16),
                vmem((heads, nc, row_dev, hd), BF16),
                vmem((2, rows, width), BF16),
                dma((7,)),
                dma((5,)),
                dma((5,)),
                dma((2 * nc,)),
                dma((nc,)),
                dma((nc,)),
                dma((nc,)),
                dma,
                dma,
                dma((2 * nc,)),
                dma((2 * nc,)),
                dma((nc,)),
                dma((2 * nc,)),
                dma,
                pltpu.SemaphoreType.REGULAR,
                pltpu.SemaphoreType.REGULAR,
            ],
            compiler_params=pltpu.CompilerParams(collective_id=0, has_side_effects=True),
        )(
            hidden,
            norm_gain,
            query_weight[0],
            query_bias,
            kv_weight[0].T,
            out_weight[0],
            kv_pool[0],
            page_table,
            context_len,
        )

    tensor = "tensor"
    return jax.shard_map(
        step,
        mesh=mesh,
        in_specs=(
            P("groups", tensor),
            P("section", None),
            P("section", None, tensor),
            P("section", tensor),
            P("section", None, tensor),
            P("section", None, tensor),
            P("section", ("groups", tensor), None, None),
            P(("groups", tensor), None),
            P(("groups", tensor)),
        ),
        out_specs=P(("groups", "section"), tensor),
        check_vma=False,
    )
```

profile of v0, /device:TPU:65, one launch (start us, length us, event | category | flops | bytes accessed | tf_op | source)
XLA Modules:
  0.0 341.1 jit_solution(11576520750244557845)
XLA Ops:
  0.0 339.9 %shard_map.91 = bf16[8,256]{1,0:T(8,128)(2,1)} custom-call(bf16[64,256]{1,0:T(8,128)(2,1)} %hidden_hbm.1, bf16[1,8192]{1,0:T(2,128)(2,1)} %gain_hbm.1, bf16[8192,128]{1,0:T(8,128)(2,1)} %bitcast.6, bf16[1,128]{1,0:T(2,128)(2,1)} %bias_hbm.1, bf16[32,8192]{1,0:T(8,128)(2,1)} %bitcast.8, bf16[4096,256]{1,0:T(8,128)(2,1)} %bitcast.7, ...), custom_call_target="tpu_custom_call" | custom-call | tf_op jit(solution)/shard_map/pallas_call | solution.py:431
  339.9 1.3 copy.11
where the time goes:
time: 341 us
  Pallas kernels  340 us (100%)
    pallas_call x1, Pallas kernels, step(): pl.pallas_call(functools.partial(kernel, nc, nsec), out_shape=jax.ShapeDt...  340 us

commit v1 on v0

--- a/solution.py
+++ b/solution.py
@@ -222,29 +222,23 @@
         n = ref.shape[0] // 2
         return ref.at[pl.ds(0 if s == 1 else n, n)]
 
-    def arrivals(known):
-        at = dict(known)
-        for d in sorted(parent):
-            if d not in at:
-                at[d] = at[parent[d]] + 1.7 + 0.6 * (d - parent[d])
-        return at
-
-    ring = [(d, s) for d in range(1, half) for s in (1, -1)] + [(half, 1)]
-
-    def relay(place, recv, sems, items, skip, use):
-        sent = []
-        for _, d, s in sorted(items):
+    ring = [(far, 1), (far, -1)]
+    ring += [(d, s) for d in range(1, half) if d != far for s in (1, -1)] + [(half, 1)]
+
+    def relay(place, recv, sems, items, direct, use):
+        sent, passed = [], []
+        for d, s in items:
             chip = chip_at(d, s)
             block = place(chip)
             wait_for(block, recv.at[chip])
-            for way in (1, -1) if d == 0 else (s,):
-                for c in kids[d]:
-                    if (d, c) not in skip:
-                        piece = in_half(block, way) if c == half else block
-                        sent.append(
-                            put(piece, piece, sems.at[len(sent)], recv.at[chip], dev(z + way * (c - d)))
-                        )
-            use(chip)
+            if d != far and passed:
+                use(passed)
+                passed = []
+            passed.append(chip)
+            for c in kids[d] if (d, s) not in direct else []:
+                piece = in_half(block, s) if c == half else block
+                sent.append(put(piece, piece, sems.at[len(sent)], recv.at[chip], dev(z + s * (c - d))))
+        use(passed)
         return sent
 
     sums = {
@@ -253,7 +247,11 @@
         "squares": jnp.zeros((rows, width), F32),
     }
 
-    def project(chip):
+    def project(chips):
+        for chip in chips:
+            project_one(chip)
+
+    def project_one(chip):
         parts = []
         for c in range(2):
             x = xbuf[chip, c].astype(F32)
@@ -266,10 +264,8 @@
             y, wkv[:, pl.ds(at, 2 * width)], (((1,), (1,)), ((), ())), preferred_element_type=F32
         )
 
-    due = arrivals({d: 1.7 + 0.6 * d for d in range(far + 1)})
-    direct = {(0, d) for d in range(1, far + 1)}
     x_sent = relay(
-        lambda c: xbuf.at[c], x_recv, x_send, [(due[d], d, s) for d, s in [(0, 1)] + ring], direct, project
+        lambda c: xbuf.at[c], x_recv, x_send, ring[:2] + [(0, 1)] + ring[2:], [(0, 1)], project
     )
 
     @pl.when(jnp.logical_and(sec == 0, core == 0))
@@ -288,9 +284,8 @@
     kv = pltpu.roll(kv, lax.rem(z, hd // part) * part, 1)
     qkv_out[per_chip] = kv.astype(BF16)
 
-    @pl.loop(0, nc - 1)
-    def _(i):
-        c = lax.rem(z + half + (1 - 2 * lax.rem(i, 2)) * ((i + 1) // 2) + nc, nc)
+    for i in range(nc - 1):
+        c = lax.rem(z + half + (1 - 2 * (i % 2)) * ((i + 1) // 2) + nc, nc)
         put(mine(qkv_out, c), mine(qkv_in, z), a2a_send, a2a_recv, dev(c))
 
     pltpu.make_async_copy(mine(qkv_out, z), mine(qkv_in, z), a2a_recv).start()
@@ -339,8 +334,7 @@
         for s in (1, -1):
             m_sent.append(put(mix_own, mix_place(z), m_root.at[len(m_sent)], m_recv.at[z], dev(z + s * c)))
     pltpu.make_async_copy(mix_own, mix_place(z), m_recv.at[z]).start()
-    due = arrivals({0: 0.0})
-    m_sent += relay(mix_place, m_recv, m_send, [(due[d], d, s) for d, s in ring], {}, lambda c: None)
+    m_sent += relay(mix_place, m_recv, m_send, ring, [], lambda chips: None)
     wait_for(mix_place(z), m_recv.at[z])
 
     own_loads[4].wait()

time: 341 us -> 320 us (0.938)
  Pallas kernels: 340 us -> 319 us
    pallas_call x1, Pallas kernels: 340 us -> 319 us  [step(): pl.pallas_call(functools.partial(kernel, nc, nsec), out_shape=jax.ShapeDt...]
where the time goes in v1:
time: 320 us
  Pallas kernels  319 us (100%)
    pallas_call x1, Pallas kernels, step(): pl.pallas_call(functools.partial(kernel, nc, nsec), out_shape=jax.ShapeDt...  319 us

profile of v1, /device:TPU:65, one launch (start us, length us, event | category | flops | bytes accessed | tf_op | source)
XLA Modules:
  0.0 320.3 jit_solution(18026958704590372489)
XLA Ops:
  0.0 319.0 %shard_map.91 = bf16[8,256]{1,0:T(8,128)(2,1)} custom-call(bf16[64,256]{1,0:T(8,128)(2,1)} %hidden_hbm.1, bf16[1,8192]{1,0:T(2,128)(2,1)} %gain_hbm.1, bf16[8192,128]{1,0:T(8,128)(2,1)} %bitcast.6, bf16[1,128]{1,0:T(2,128)(2,1)} %bias_hbm.1, bf16[32,8192]{1,0:T(8,128)(2,1)} %bitcast.8, bf16[4096,256]{1,0:T(8,128)(2,1)} %bitcast.7, ...), custom_call_target="tpu_custom_call" | custom-call | tf_op jit(solution)/shard_map/pallas_call | solution.py:425
  319.0 1.3 copy.11

commit v2 on v1

--- a/solution.py
+++ b/solution.py
@@ -72,11 +72,11 @@
     row_dev, blocks = table_ref.shape
     width = hid.shape[2]
     rows = nc * row_dev
-    hd = keys.shape[1]
+    hd = keys.shape[2]
     heads = mix_own.shape[0]
     page_len = pool.shape[1]
     span = page_len * blocks
-    wide = keys.shape[0]
+    wide = keys.shape[1]
     kvh = wide // row_dev // span
     per_chip = heads // nc
     part = wkv.shape[0]
@@ -91,12 +91,23 @@
     z = me // 2
     core = lax.rem(me, 2)
     last = nsec - 1
+    turnover = nsec // 2
+    flip = sec // turnover
+    piece = lax.rem(core + flip, 2)
 
     def dev(zz, s=None):
         where = {"tensor": lax.rem(zz + 2 * nc, nc) * 2 + core}
         if s is not None:
             where["section"] = s
         return where
+
+    def ahead(zz):
+        other = lax.rem(core + (sec + 1) // turnover + flip, 2)
+        return {"tensor": lax.rem(zz + 2 * nc, nc) * 2 + other, "section": sec + 1}
+
+    def behind(zz):
+        other = lax.rem(core + (sec - 1) // turnover + flip, 2)
+        return {"tensor": lax.rem(zz + 2 * nc, nc) * 2 + other, "section": sec - 1}
 
     def put(src, dst, ssem, rsem, where):
         copy = pltpu.make_async_remote_copy(
@@ -141,13 +152,13 @@
     @pl.when(sec < last)
     def _():
         for s, d in near:
-            greet(dev(z + s * d, sec + 1))
+            greet(ahead(z + s * d))
 
     @pl.when(sec > 0)
     def _():
         pl.semaphore_wait(barrier, nc + len(near))
         for s, d in near:
-            pl.semaphore_signal(ready, inc=1, device_id=dev(z - s * d, sec - 1), device_id_type=MESH)
+            pl.semaphore_signal(ready, inc=1, device_id=behind(z - s * d), device_id_type=MESH)
 
     @pl.when(sec == 0)
     def _():
@@ -158,11 +169,8 @@
         for k, (src, dst) in enumerate(zip(sources, shares(core)))
     ]
 
-    def send_stream(src, section, sems):
-        return [
-            put(src, xbuf.at[z], sems.at[k], x_recv.at[z], dev(z + s * d, section) if d else dev(z, section))
-            for k, (s, d) in enumerate(near)
-        ]
+    def send_stream(src, sems):
+        return [put(src, xbuf.at[z], sems.at[k], x_recv.at[z], ahead(z + s * d)) for k, (s, d) in enumerate(near)]
 
     own_loads[0].wait()
     wait_for(hid.at[0], push_recv.at[0])
@@ -195,8 +203,8 @@
             page = pool[lax.rem(table_ref[r, b], pool.shape[0])]
             for k in range(kvh):
                 at = (r * kvh + k) * span + b * page_len
-                keys[at : at + page_len, :] = page[:, k * hd : (k + 1) * hd]
-                values[at : at + page_len, :] = page[:, (kvh + k) * hd : (kvh + k + 1) * hd]
+                keys[0, at : at + page_len, :] = page[:, k * hd : (k + 1) * hd]
+                values[0, at : at + page_len, :] = page[:, (kvh + k) * hd : (kvh + k + 1) * hd]
 
     q_rows = per_chip * rows
     lane = lax.broadcasted_iota(jnp.int32, (q_rows, hd), 1)
@@ -208,9 +216,16 @@
     frequency = jnp.exp(lax.rem(lane, hd // 2).astype(F32) * (-2.0 * LOG_ROPE_BASE / hd))
     angle = position * frequency
     sine = jnp.sin(angle)
-    cos_tab[...] = jnp.cos(angle)
-    sin_tab[...] = jnp.where(lane < hd // 2, -sine, sine)
-    lim_tab[...] = position
+    cos_tab[0] = jnp.cos(angle)
+    sin_tab[0] = jnp.where(lane < hd // 2, -sine, sine)
+    lim_tab[0] = position
+    tables = [keys, values, cos_tab, sin_tab, lim_tab]
+
+    @pl.when(flip == 1)
+    def _():
+        for k, table in enumerate(tables):
+            put(table.at[0], table.at[1], push_send.at[len(sources) + k], push_recv.at[len(sources) + k], sibling)
+
     for k in range(1, 4):
         own_loads[k].wait()
         wait_for(shares(0)[k], push_recv.at[k])
@@ -225,13 +240,21 @@
     ring = [(far, 1), (far, -1)]
     ring += [(d, s) for d in range(1, half) if d != far for s in (1, -1)] + [(half, 1)]
 
-    def relay(place, recv, sems, items, direct, use):
+    def pass_turn():
+        @pl.when(jnp.logical_and(sec == 0, core == 0))
+        def _():
+            pl.semaphore_signal(turn, inc=1, device_id=sibling, device_id_type=MESH)
+
+    def relay(place, recv, sems, items, direct, use, after_far=None):
         sent, passed = [], []
         for d, s in items:
             chip = chip_at(d, s)
             block = place(chip)
             wait_for(block, recv.at[chip])
             if d != far and passed:
+                if after_far:
+                    after_far()
+                    after_far = None
                 use(passed)
                 passed = []
             passed.append(chip)
@@ -268,10 +291,6 @@
         lambda c: xbuf.at[c], x_recv, x_send, ring[:2] + [(0, 1)] + ring[2:], [(0, 1)], project
     )
 
-    @pl.when(jnp.logical_and(sec == 0, core == 0))
-    def _():
-        pl.semaphore_signal(turn, inc=1, device_id=sibling, device_id_type=MESH)
-
     def mine(ref, c):
         return ref.at[:, pl.ds(c * row_dev, row_dev)]
 
@@ -289,6 +308,12 @@
         put(mine(qkv_out, c), mine(qkv_in, z), a2a_send, a2a_recv, dev(c))
 
     pltpu.make_async_copy(mine(qkv_out, z), mine(qkv_in, z), a2a_recv).start()
+    pass_turn()
+
+    @pl.when(flip == 1)
+    def _():
+        for k, table in enumerate(tables):
+            wait_for(table.at[1], push_recv.at[len(sources) + k])
 
     def grid(shape, axis):
         return lax.broadcasted_iota(jnp.int32, shape, axis)
@@ -297,7 +322,7 @@
     q_of, c_of = grid((q_rows, wide), 0), grid((q_rows, wide), 1)
     key_head = (lax.rem(q_of, rows) // row_dev * per_chip + q_of // rows) // group
     matching = c_of // span == lax.rem(q_of, row_dev) * kvh + key_head
-    usable = matching & (lax.rem(c_of, span).astype(F32) < lim_tab[:, :1])
+    usable = matching & (lax.rem(c_of, span).astype(F32) < lim_tab[flip][:, :1])
     s_row, s_col = grid((q_rows, rows), 0), grid((q_rows, rows), 1)
     same = lax.rem(s_row, row_dev) == lax.rem(s_col, row_dev)
     source = s_col // row_dev // (hd // part)
@@ -305,7 +330,7 @@
     pick_key = jnp.where(same & (source == wanted), 1.0, 0.0).astype(BF16)
     pick_value = jnp.where(same & (source == wanted + kvh), 1.0, 0.0).astype(BF16)
     root = hd ** (-0.5)
-    cos, sin = cos_tab[...], sin_tab[...]
+    cos, sin = cos_tab[flip], sin_tab[flip]
     wait_for(qkv_in, a2a_recv)
 
     def rotate(v):
@@ -315,7 +340,7 @@
     fresh = qkv_in[per_chip]
     key_new = rotate(jnp.dot(pick_key, fresh, preferred_element_type=F32))
     value_new = jnp.dot(pick_value, fresh, preferred_element_type=F32)
-    scores = lax.dot_general(rotated, keys[...], (((1,), (1,)), ((), ())), preferred_element_type=F32) * root
+    scores = lax.dot_general(rotated, keys[flip], (((1,), (1,)), ((), ())), preferred_element_type=F32) * root
     own_score = jnp.sum(rotated.astype(F32) * key_new.astype(F32), axis=1, keepdims=True) * root
     top = jnp.maximum(jnp.max(jnp.where(usable, scores, -1e30), axis=1, keepdims=True), own_score)
     weights = jnp.where(usable, jnp.exp(scores - top), 0.0)
@@ -323,7 +348,7 @@
     total = jnp.sum(weights, axis=1, keepdims=True) + own_weight
     weights = (weights / total).astype(BF16)
     own_weight = (own_weight / total).astype(BF16).astype(F32)
-    mixture = jnp.dot(weights, values[...], preferred_element_type=F32) + own_weight * value_new
+    mixture = jnp.dot(weights, values[flip], preferred_element_type=F32) + own_weight * value_new
     mix_own[...] = mixture.astype(BF16).reshape(heads, row_dev, hd)
 
     def mix_place(c):
@@ -351,7 +376,7 @@
     @pl.when(sec < last)
     def _():
         pl.semaphore_wait(ready, len(near))
-        for copy in send_stream(stream, sec + 1, r_send):
+        for copy in send_stream(stream, r_send):
             copy.wait_send()
 
     @pl.when(sec == last)
@@ -359,7 +384,7 @@
         def share(s, c, j):
             return (
                 stream.at[c, pl.ds((s * chips + j) * row_dev, row_dev)],
-                out_ref.at[pl.ds((j * 2 + core) * row_dev, row_dev)],
+                out_ref.at[pl.ds((j * 2 + piece) * row_dev, row_dev)],
             )
 
         def sem_of(s, c, j):
@@ -396,6 +421,11 @@
         for k, (s, d) in enumerate(near):
             if d:
                 wait_for(first, i_send.at[k])
+
+    @pl.when(flip == 1)
+    def _():
+        for k, table in enumerate(tables):
+            wait_for(table.at[0], push_send.at[len(sources) + k])
 
     others = pl.ds(0, rows - row_dev)
     wait_for(qkv_out.at[:, others], a2a_send)
@@ -436,11 +466,11 @@
                 vmem((part, features), BF16),
                 vmem((heads * hd, 2 * width), BF16),
                 vmem((pages, page_len, kv_width), BF16),
-                vmem((cached, hd), BF16),
-                vmem((cached, hd), BF16),
-                vmem((q_rows, hd), F32),
-                vmem((q_rows, hd), F32),
-                vmem((q_rows, hd), F32),
+                vmem((2, cached, hd), BF16),
+                vmem((2, cached, hd), BF16),
+                vmem((2, q_rows, hd), F32),
+                vmem((2, q_rows, hd), F32),
+                vmem((2, q_rows, hd), F32),
                 vmem((2, rows, width), BF16),
                 vmem((nc, 2, rows, width), BF16),
                 vmem((3, rows, hd), BF16),
@@ -449,8 +479,8 @@
                 vmem((heads, nc, row_dev, hd), BF16),
                 vmem((2, rows, width), BF16),
                 dma((7,)),
-                dma((5,)),
-                dma((5,)),
+                dma((10,)),
+                dma((10,)),
                 dma((2 * nc,)),
                 dma((nc,)),
                 dma((nc,)),

time: 320 us -> 317 us (level)
  no operation moved by 1% of the time
where the time goes in v2:
time: 317 us
  Pallas kernels  316 us (100%)
    pallas_call x1, Pallas kernels, step(): pl.pallas_call(functools.partial(kernel, nc, nsec), out_shape=jax.ShapeDt...  316 us

profile of v2, /device:TPU:65, one launch (start us, length us, event | category | flops | bytes accessed | tf_op | source)
XLA Modules:
  0.0 317.2 jit_solution(14870460741047925501)
XLA Ops:
  0.0 316.0 %shard_map.91 = bf16[8,256]{1,0:T(8,128)(2,1)} custom-call(bf16[64,256]{1,0:T(8,128)(2,1)} %hidden_hbm.1, bf16[1,8192]{1,0:T(2,128)(2,1)} %gain_hbm.1, bf16[8192,128]{1,0:T(8,128)(2,1)} %bitcast.6, bf16[1,128]{1,0:T(2,128)(2,1)} %bias_hbm.1, bf16[32,8192]{1,0:T(8,128)(2,1)} %bitcast.8, bf16[4096,256]{1,0:T(8,128)(2,1)} %bitcast.7, ...), custom_call_target="tpu_custom_call" | custom-call | tf_op jit(solution)/shard_map/pallas_call | solution.py:455
  316.0 1.3 copy.11

commit v3 on v2

--- a/solution.py
+++ b/solution.py
@@ -91,8 +91,7 @@
     z = me // 2
     core = lax.rem(me, 2)
     last = nsec - 1
-    turnover = nsec // 2
-    flip = sec // turnover
+    flip = lax.rem(sec, 2)
     piece = lax.rem(core + flip, 2)
 
     def dev(zz, s=None):
@@ -102,12 +101,10 @@
         return where
 
     def ahead(zz):
-        other = lax.rem(core + (sec + 1) // turnover + flip, 2)
-        return {"tensor": lax.rem(zz + 2 * nc, nc) * 2 + other, "section": sec + 1}
+        return {"tensor": lax.rem(zz + 2 * nc, nc) * 2 + 1 - core, "section": sec + 1}
 
     def behind(zz):
-        other = lax.rem(core + (sec - 1) // turnover + flip, 2)
-        return {"tensor": lax.rem(zz + 2 * nc, nc) * 2 + other, "section": sec - 1}
+        return {"tensor": lax.rem(zz + 2 * nc, nc) * 2 + 1 - core, "section": sec - 1}
 
     def put(src, dst, ssem, rsem, where):
         copy = pltpu.make_async_remote_copy(

time: 317 us -> 318 us (level)
  no operation moved by 1% of the time
where the time goes in v3:
time: 318 us
  Pallas kernels  317 us (100%)
    pallas_call x1, Pallas kernels, step(): pl.pallas_call(functools.partial(kernel, nc, nsec), out_shape=jax.ShapeDt...  317 us

profile of v3, /device:TPU:65, one launch (start us, length us, event | category | flops | bytes accessed | tf_op | source)
XLA Modules:
  0.0 317.8 jit_solution(526483063785752384)
XLA Ops:
  0.0 316.5 %shard_map.91 = bf16[8,256]{1,0:T(8,128)(2,1)} custom-call(bf16[64,256]{1,0:T(8,128)(2,1)} %hidden_hbm.1, bf16[1,8192]{1,0:T(2,128)(2,1)} %gain_hbm.1, bf16[8192,128]{1,0:T(8,128)(2,1)} %bitcast.6, bf16[1,128]{1,0:T(2,128)(2,1)} %bias_hbm.1, bf16[32,8192]{1,0:T(8,128)(2,1)} %bitcast.8, bf16[4096,256]{1,0:T(8,128)(2,1)} %bitcast.7, ...), custom_call_target="tpu_custom_call" | custom-call | tf_op jit(solution)/shard_map/pallas_call | solution.py:452
  316.5 1.3 copy.11

commit v4 on v3

--- a/solution.py
+++ b/solution.py
@@ -285,7 +285,7 @@
         )
 
     x_sent = relay(
-        lambda c: xbuf.at[c], x_recv, x_send, ring[:2] + [(0, 1)] + ring[2:], [(0, 1)], project
+        lambda c: xbuf.at[c], x_recv, x_send, ring[:2] + [(0, 1)] + ring[2:], [(0, 1)], project, pass_turn
     )
 
     def mine(ref, c):
@@ -305,7 +305,6 @@
         put(mine(qkv_out, c), mine(qkv_in, z), a2a_send, a2a_recv, dev(c))
 
     pltpu.make_async_copy(mine(qkv_out, z), mine(qkv_in, z), a2a_recv).start()
-    pass_turn()
 
     @pl.when(flip == 1)
     def _():

time: 318 us -> 315 us (level)
  Pallas kernels: 317 us -> 313 us
where the time goes in v4:
time: 315 us
  Pallas kernels  313 us (99%)
    pallas_call x1, Pallas kernels, step(): pl.pallas_call(functools.partial(kernel, nc, nsec), out_shape=jax.ShapeDt...  313 us

profile of v4, /device:TPU:65, one launch (start us, length us, event | category | flops | bytes accessed | tf_op | source)
XLA Modules:
  0.0 314.8 jit_solution(71840710627712618)
XLA Ops:
  0.0 313.5 %shard_map.91 = bf16[8,256]{1,0:T(8,128)(2,1)} custom-call(bf16[64,256]{1,0:T(8,128)(2,1)} %hidden_hbm.1, bf16[1,8192]{1,0:T(2,128)(2,1)} %gain_hbm.1, bf16[8192,128]{1,0:T(8,128)(2,1)} %bitcast.6, bf16[1,128]{1,0:T(2,128)(2,1)} %bias_hbm.1, bf16[32,8192]{1,0:T(8,128)(2,1)} %bitcast.8, bf16[4096,256]{1,0:T(8,128)(2,1)} %bitcast.7, ...), custom_call_target="tpu_custom_call" | custom-call | tf_op jit(solution)/shard_map/pallas_call | solution.py:451
  313.5 1.3 copy.11
